TPU v7x, 32 devices: a whole 2x2x4 slice. The times are simulated.
32 devices in a mesh: groups: 2 (over y), seq: 4 (over z), head: 2 (over x), inner: 2 (over core).
Axes of the slice: x: 2, y: 2, z: 4, core: 2. Of those that a mesh axis runs over, the one named last changes fastest.
Arguments:
- queries: bfloat16 [4096, 2, 8, 128], P(('groups', 'seq'), 'head', 'inner'), parts along dimension 0, may hold values from -120 to 120
- grad_out: bfloat16 [4096, 2, 8, 128], P(('groups', 'seq'), 'head', 'inner'), parts along dimension 0, may hold values from -6 to 6
- keys: bfloat16 [4096, 2, 128], P(('groups', 'seq'), 'head'), parts along dimension 0, may hold values from -6 to 6
- values: bfloat16 [4096, 2, 128], P(('groups', 'seq'), 'head'), parts along dimension 0, may hold values from -6 to 6
- indices: int32 [2, 64, 16], P('head', 'groups'), parts along dimension 1, may hold values from 0 to 31, as said below
- valid: int32 [2, 64, 16], P('head', 'groups'), parts along dimension 1, may hold values from 0 to 1
Outputs:
- grad_queries: bfloat16 [4096, 2, 8, 128], P(('groups', 'seq'), 'head', 'inner'), parts along dimension 0
- grad_keys: bfloat16 [4096, 2, 128], P(('groups', 'seq'), 'head'), parts along dimension 0
- grad_values: bfloat16 [4096, 2, 128], P(('groups', 'seq'), 'head'), parts along dimension 0
There are 2 independent parts, one for each index of `groups`. A program takes and returns all parts, laid end to end along the dimension named above; each array names one. Nothing has to cross between parts.
Inputs may be any that keep to these rules, and one draw needn't show every extreme that they name: `indices`: call blocks r * 8 to r * 8 + 7 run r. For every KV head and query block b: slot 0 names b and is valid; the valid slots name distinct blocks at most b; over all query blocks of run r, the valid slots name blocks of runs later than r never, and for each earlier run exactly 4 distinct blocks of it. Slots that are not valid name arbitrary blocks.
All inputs are finite; a program needn't handle non-finite values.
Results may differ from a plain program's by a relative error of at most 0.007.
Values may be sent and summed in bfloat16 or wider, within the bound.
No kernel may reach another device: no remote copies, remote signals or barrier semaphores. Data moves between devices by JAX's collectives and lax.ppermute only.
A program may use at most 64 MiB of HBM per device.

v0:
```python
import math
import jax
import jax.numpy as jnp
from jax import lax
from jax.sharding import PartitionSpec as P

BLK = 64
TOPK = 16
CAP = 4


def per_device(queries, grad_out, keys, values, indices, valid):
    tokens = queries.shape[0]
    heads_here = queries.shape[2]
    width = queries.shape[3]
    seq_count = lax.axis_size("seq")
    seq_here = lax.axis_index("seq")
    blocks_here = tokens // BLK
    total_blocks = indices.shape[1]
    scaling = 1.0 / math.sqrt(width)
    remote_rows = seq_count * CAP
    dest_rows = remote_rows + blocks_here
    picks_all = indices[0]
    valid_all = valid[0] > 0
    owner_all = picks_all // blocks_here
    local_all = picks_all % blocks_here
    my_picks = lax.dynamic_slice_in_dim(picks_all, seq_here * blocks_here, blocks_here, 0)
    my_valid = lax.dynamic_slice_in_dim(valid_all, seq_here * blocks_here, blocks_here, 0)
    my_owner = my_picks // blocks_here
    my_local = my_picks % blocks_here
    remote = my_valid & (my_owner != seq_here)
    block_ids = jnp.arange(total_blocks, dtype=jnp.int32)
    hits_in = (my_picks[:, :, None] == block_ids[None, None, :]) & remote[:, :, None]
    present_in = jnp.any(hits_in, axis=(0, 1)).reshape(seq_count, blocks_here)
    rank_in = jnp.cumsum(present_in.astype(jnp.int32), axis=1) - 1
    slot_ref = jnp.sum(jnp.where(hits_in, rank_in.reshape(-1)[None, None, :], 0), axis=2)
    row_index = jnp.where(remote, my_owner * CAP + slot_ref, remote_rows + my_local)
    source_run = block_ids // blocks_here
    incoming = valid_all & (owner_all == seq_here) & (source_run != seq_here)[:, None]
    hits_out = (
        local_all[:, :, None] == jnp.arange(blocks_here, dtype=jnp.int32)[None, None, :]
    ) & incoming[:, :, None]
    present_out = jnp.any(hits_out.reshape(seq_count, blocks_here * TOPK, blocks_here), axis=1)
    rank_out = jnp.cumsum(present_out.astype(jnp.int32), axis=1) - 1
    choose_out = present_out[:, None, :] & (
        rank_out[:, None, :] == jnp.arange(CAP, dtype=jnp.int32)[None, :, None]
    )
    wanted = my_picks.reshape(-1)
    blank = jnp.zeros((blocks_here * TOPK, BLK, width), jnp.bfloat16)
    carry = (blank, blank)
    key_piece = lax.all_gather(keys, "seq", axis=0, tiled=True)
    value_piece = lax.all_gather(values, "seq", axis=0, tiled=True)
    count = key_piece.shape[0] // BLK
    relative = wanted
    inside = (relative >= 0) & (relative < count)
    relative = jnp.clip(relative, 0, count - 1)
    key_rows = jnp.take(key_piece[:, 0].reshape(count, BLK, width), relative, axis=0)
    value_rows = jnp.take(value_piece[:, 0].reshape(count, BLK, width), relative, axis=0)
    sel_keys = jnp.where(inside[:, None, None], key_rows, carry[0])
    sel_values = jnp.where(inside[:, None, None], value_rows, carry[1])
    group = math.gcd(blocks_here, max(1, 512 // (BLK * heads_here)))
    steps_count = blocks_here // group
    span = TOPK * BLK
    position = jnp.arange(BLK, dtype=jnp.int32)
    causal = position[None, :] <= position[:, None]
    block_global = seq_here * blocks_here + jnp.arange(blocks_here, dtype=jnp.int32)
    before = my_picks < block_global[:, None]
    same = my_picks == block_global[:, None]
    allowed = my_valid[:, None, :, None] & (
        before[:, None, :, None] | same[:, None, :, None] & causal[None, :, None, :]
    )
    allowed = allowed.reshape(steps_count, group, BLK, span)
    query_steps = queries[:, 0].reshape(steps_count, group, BLK, heads_here, width)
    grad_steps = grad_out[:, 0].reshape(steps_count, group, BLK, heads_here, width)
    key_steps = sel_keys.reshape(steps_count, group, span, width)
    value_steps = sel_values.reshape(steps_count, group, span, width)
    row_steps = row_index.reshape(steps_count, group * TOPK)

    def attend(carry, inputs):
        key_acc, value_acc = carry
        q_group, do_group, k_group, v_group, mask_group, rows_group = inputs
        mask_heads = mask_group[:, None, :, :]
        scores = (
            jnp.einsum("qigw,qsw->qgis", q_group, k_group, preferred_element_type=jnp.float32)
            * scaling
        )
        highest = jnp.max(jnp.where(mask_heads, scores, -jnp.inf), axis=-1, keepdims=True)
        weights = jnp.where(mask_heads, jnp.exp(scores - highest), 0.0)
        probs = weights / jnp.sum(weights, axis=-1, keepdims=True)
        probs_b = probs.astype(jnp.bfloat16)
        dprobs = jnp.einsum("qigw,qsw->qgis", do_group, v_group, preferred_element_type=jnp.float32)
        delta = jnp.sum(probs * dprobs, axis=-1, keepdims=True)
        dscores = (probs * (dprobs - delta)).astype(jnp.bfloat16)
        query_grad = (
            jnp.einsum("qgis,qsw->qigw", dscores, k_group, preferred_element_type=jnp.float32)
            * scaling
        ).astype(jnp.bfloat16)
        key_terms = (
            jnp.einsum("qgis,qigw->qsw", dscores, q_group, preferred_element_type=jnp.float32)
            * scaling
        )
        value_terms = jnp.einsum(
            "qgis,qigw->qsw", probs_b, do_group, preferred_element_type=jnp.float32
        )
        key_acc = key_acc.at[rows_group].add(key_terms.reshape(group * TOPK, BLK * width))
        value_acc = value_acc.at[rows_group].add(value_terms.reshape(group * TOPK, BLK * width))
        return ((key_acc, value_acc), query_grad)

    zeros_dest = jnp.zeros((dest_rows, BLK * width), jnp.float32)
    (key_acc, value_acc), query_grads = lax.scan(
        attend,
        (zeros_dest, zeros_dest),
        (query_steps, grad_steps, key_steps, value_steps, allowed, row_steps),
    )
    grad_queries = query_grads.reshape(tokens, 1, heads_here, width)
    send_key_tiles = key_acc[:remote_rows].reshape(seq_count, CAP, BLK * width)
    send_value_tiles = value_acc[:remote_rows].reshape(seq_count, CAP, BLK * width)
    own_keys = key_acc[remote_rows:]
    own_values = value_acc[remote_rows:]
    choose_float = choose_out.astype(jnp.float32)
    back_keys, back_values = (
        lax.all_to_all(send_key_tiles, "seq", split_axis=0, concat_axis=0, tiled=True),
        lax.all_to_all(send_value_tiles, "seq", split_axis=0, concat_axis=0, tiled=True),
    )
    local_keys = own_keys + jnp.einsum(
        "dcb,dcx->bx", choose_float, back_keys, precision=lax.Precision.HIGHEST
    )
    local_values = own_values + jnp.einsum(
        "dcb,dcx->bx", choose_float, back_values, precision=lax.Precision.HIGHEST
    )
    total_keys, total_values = lax.psum((local_keys, local_values), "inner")
    grad_keys = total_keys.astype(jnp.bfloat16).reshape(tokens, 1, width)
    grad_values = total_values.astype(jnp.bfloat16).reshape(tokens, 1, width)
    return (grad_queries, grad_keys, grad_values)


def solution(mesh):
    return jax.shard_map(
        per_device,
        mesh=mesh,
        in_specs=(
            P(("groups", "seq"), "head", "inner", None),
            P(("groups", "seq"), "head", "inner", None),
            P(("groups", "seq"), "head", None),
            P(("groups", "seq"), "head", None),
            P("head", "groups", None),
            P("head", "groups", None),
        ),
        out_specs=(
            P(("groups", "seq"), "head", "inner", None),
            P(("groups", "seq"), "head", None),
            P(("groups", "seq"), "head", None),
        ),
        check_vma=False,
    )
```

profile of v0, /device:TPU:0, one launch (start us, length us, event | category | flops | bytes accessed | tf_op | source)
XLA Modules:
  0.0 166.9 jit_solution(11409170172867323838)
XLA Ops:
  4.3 17.6 %all_gather.6 = bf16[2048,1,128]{2,0,1:T(8,128)(2,1)S(1)} all-gather(bf16[512,1,128]{2,0,1:T(8,128)(2,1)} %param.12), channel_id=1, replica_groups=mesh['groups'=2,'seq'=4,'head'=2,'inner'=2] {'seq'}, dimensions={0}, use_global_device_ids=true | all-gather | bytes 655360 | tf_op jit(solution)/shard_map/all_gather | solution.py:51
  21.9 16.6 %all_gather.7 = bf16[2048,1,128]{2,0,1:T(8,128)(2,1)S(1)} all-gather(bf16[512,1,128]{2,0,1:T(8,128)(2,1)} %param.13), channel_id=1, replica_groups=mesh['groups'=2,'seq'=4,'head'=2,'inner'=2] {'seq'}, dimensions={0}, use_global_device_ids=true | all-gather | bytes 655360 | tf_op jit(solution)/shard_map/all_gather | solution.py:52
  39.4 2.1 %gather_fusion = bf16[128,64,128]{2,1,0:T(8,128)(2,1)} fusion(bf16[32,64,128]{2,1,0:T(8,128)(2,1)S(1)} %bitcast.131, s32[1024]{0:T(1024)S(1)} %pad_clamp_fusion), kind=kCustom, calls=%fused_computation.clone | custom fusion | bytes 4194816 | tf_op jit(solution)/shard_map/jit(_take)/gather | solution.py:57
  42.8 3.7 %select_select_fusion = (bf16[128,64,128]{2,1,0:T(8,128)(2,1)}, bf16[128,64,128]{2,1,0:T(8,128)(2,1)}) fusion(bf16[128,64,128]{2,1,0:T(8,128)(2,1)S(1)} %gather_fusion.1, pred[128]{0:T(512)(128)(4,1)S(1)} %compare_and_fusion.2, pred[128]{0:T(512)(128)(4,1)S(1)} %and.166, bf16[128,64,128]{2,1,0:T(8,128)(2,1)} %gather_fusion), kind=kLoop, calls=%fused_computation.54 | loop fusion | flops 4194304 | bytes 8388864 | tf_op jit(solution)/shard_map/jit(_where)/select_n | solution.py:60
  46.6 84.0 %while.14 = (s32[]{:T(128)}, f32[24,8192]{1,0:T(8,128)S(1)}, f32[24,8192]{1,0:T(8,128)S(1)}, bf16[4,2,64,4,128]{4,3,2,1,0:T(4,128)(2,1)}, s32[4,32]{1,0:T(4,128)...) while((s32[]{:T(128)}, f32[24,8192]{1,0:T(8,128)S(1)}, ...), condition=%wide.region_9.11_spmd, body=%wide.region_3.10_spmd.sunk | while | flops 679871104 | bytes 52703944 | solution.py:110
  52.2 1.7 %convolution_bitcast_fusion.5 = f32[2,1024,128]{2,1,0:T(8,128)} fusion(bf16[1,2,64,4,128]{4,3,2,1,0:T(4,128)(2,1)S(1)} %get-tuple-element.196, f32[2,4,64,1024]{3,2,1,0:T(8,128)S(1)} %get-tuple-element.194, f32[2,4,64]{2,1,0:T(4,128)S(1)} %get-tuple-element.195), kind=kOutput, calls=%fused_computation.16.clone.1 | convolution fusion | flops 135266304 | bytes 3278848 | tf_op jit(solution)/shard_map/while/body/eval_jaxpr/qgis,qigw->qsw/dot_general | solution.py:102
  55.3 2.1 %scatter_fusion.1 = f32[24,8192]{1,0:T(8,128)S(1)} fusion(f32[24,8192]{1,0:T(8,128)S(1)} %get-tuple-element.212, s32[32]{0:T(128)S(1)} %fusion.73, f32[32,8192]{1,0:T(8,128)S(1)} %reshape.340), kind=kCustom, calls=%fused_computation.3.clone.1 | custom fusion | flops 262144 | bytes 3145856 | tf_op jit(solution)/shard_map/while/body/eval_jaxpr/scatter-add | solution.py:106
  57.4 2.4 %fusion.76 = (f32[2,4,64]{2,1,0:T(4,128)S(1)}, f32[2,1024,64,4]{1,2,3,0:T(8,128)S(1)}) fusion(f32[2,4,64,1024]{3,2,1,0:T(8,128)} %copy-done, f32[2,4,64]{2,1,0:T(4,128)S(1)} %get-tuple-element.195, bf16[1,2,64,4,128]{4,3,2,1,0:T(4,128)(2,1)S(1)} %get-tuple-element.196, bf16[4,2,1024,128]{3,2,1,0:T(8,128)(2,1)} %get-tuple-element.229, s32[]{:T(128)S(6)} %copy.84), kind=kOutput, calls=%fused_computation.7.clone.1 | convolution fusion | flops 135790080 | bytes 4853764 | tf_op jit(solution)/shard_map/while/body/eval_jaxpr/qigw,qsw->qgis/dot_general | solution.py:91
  64.7 2.1 %scatter_fusion = f32[24,8192]{1,0:T(8,128)S(1)} fusion(f32[24,8192]{1,0:T(8,128)S(1)} %get-tuple-element.211, s32[32]{0:T(128)S(1)} %fusion.73, f32[32,8192]{1,0:T(8,128)S(1)} %reshape.339), kind=kCustom, calls=%fused_computation.2.clone.1 | custom fusion | flops 262144 | bytes 3145856 | tf_op jit(solution)/shard_map/while/body/eval_jaxpr/scatter-add | solution.py:105
  73.2 1.7 %convolution_bitcast_fusion.5 = f32[2,1024,128]{2,1,0:T(8,128)} fusion(bf16[1,2,64,4,128]{4,3,2,1,0:T(4,128)(2,1)S(1)} %get-tuple-element.196, f32[2,4,64,1024]{3,2,1,0:T(8,128)S(1)} %get-tuple-element.194, f32[2,4,64]{2,1,0:T(4,128)S(1)} %get-tuple-element.195), kind=kOutput, calls=%fused_computation.16.clone.1 | convolution fusion | flops 135266304 | bytes 3278848 | tf_op jit(solution)/shard_map/while/body/eval_jaxpr/qgis,qigw->qsw/dot_general | solution.py:102
  76.3 2.1 %scatter_fusion.1 = f32[24,8192]{1,0:T(8,128)S(1)} fusion(f32[24,8192]{1,0:T(8,128)S(1)} %get-tuple-element.212, s32[32]{0:T(128)S(1)} %fusion.73, f32[32,8192]{1,0:T(8,128)S(1)} %reshape.340), kind=kCustom, calls=%fused_computation.3.clone.1 | custom fusion | flops 262144 | bytes 3145856 | tf_op jit(solution)/shard_map/while/body/eval_jaxpr/scatter-add | solution.py:106
  78.4 2.4 %fusion.76 = (f32[2,4,64]{2,1,0:T(4,128)S(1)}, f32[2,1024,64,4]{1,2,3,0:T(8,128)S(1)}) fusion(f32[2,4,64,1024]{3,2,1,0:T(8,128)} %copy-done, f32[2,4,64]{2,1,0:T(4,128)S(1)} %get-tuple-element.195, bf16[1,2,64,4,128]{4,3,2,1,0:T(4,128)(2,1)S(1)} %get-tuple-element.196, bf16[4,2,1024,128]{3,2,1,0:T(8,128)(2,1)} %get-tuple-element.229, s32[]{:T(128)S(6)} %copy.84), kind=kOutput, calls=%fused_computation.7.clone.1 | convolution fusion | flops 135790080 | bytes 4853764 | tf_op jit(solution)/shard_map/while/body/eval_jaxpr/qigw,qsw->qgis/dot_general | solution.py:91
  85.7 2.1 %scatter_fusion = f32[24,8192]{1,0:T(8,128)S(1)} fusion(f32[24,8192]{1,0:T(8,128)S(1)} %get-tuple-element.211, s32[32]{0:T(128)S(1)} %fusion.73, f32[32,8192]{1,0:T(8,128)S(1)} %reshape.339), kind=kCustom, calls=%fused_computation.2.clone.1 | custom fusion | flops 262144 | bytes 3145856 | tf_op jit(solution)/shard_map/while/body/eval_jaxpr/scatter-add | solution.py:105
  97.3 2.1 %scatter_fusion.1 = f32[24,8192]{1,0:T(8,128)S(1)} fusion(f32[24,8192]{1,0:T(8,128)S(1)} %get-tuple-element.212, s32[32]{0:T(128)S(1)} %fusion.73, f32[32,8192]{1,0:T(8,128)S(1)} %reshape.340), kind=kCustom, calls=%fused_computation.3.clone.1 | custom fusion | flops 262144 | bytes 3145856 | tf_op jit(solution)/shard_map/while/body/eval_jaxpr/scatter-add | solution.py:106
  99.4 2.4 %fusion.76 = (f32[2,4,64]{2,1,0:T(4,128)S(1)}, f32[2,1024,64,4]{1,2,3,0:T(8,128)S(1)}) fusion(f32[2,4,64,1024]{3,2,1,0:T(8,128)} %copy-done, f32[2,4,64]{2,1,0:T(4,128)S(1)} %get-tuple-element.195, bf16[1,2,64,4,128]{4,3,2,1,0:T(4,128)(2,1)S(1)} %get-tuple-element.196, bf16[4,2,1024,128]{3,2,1,0:T(8,128)(2,1)} %get-tuple-element.229, s32[]{:T(128)S(6)} %copy.84), kind=kOutput, calls=%fused_computation.7.clone.1 | convolution fusion | flops 135790080 | bytes 4853764 | tf_op jit(solution)/shard_map/while/body/eval_jaxpr/qigw,qsw->qgis/dot_general | solution.py:91
  106.7 2.1 %scatter_fusion = f32[24,8192]{1,0:T(8,128)S(1)} fusion(f32[24,8192]{1,0:T(8,128)S(1)} %get-tuple-element.211, s32[32]{0:T(128)S(1)} %fusion.73, f32[32,8192]{1,0:T(8,128)S(1)} %reshape.339), kind=kCustom, calls=%fused_computation.2.clone.1 | custom fusion | flops 262144 | bytes 3145856 | tf_op jit(solution)/shard_map/while/body/eval_jaxpr/scatter-add | solution.py:105
  118.3 2.1 %scatter_fusion.1 = f32[24,8192]{1,0:T(8,128)S(1)} fusion(f32[24,8192]{1,0:T(8,128)S(1)} %get-tuple-element.212, s32[32]{0:T(128)S(1)} %fusion.73, f32[32,8192]{1,0:T(8,128)S(1)} %reshape.340), kind=kCustom, calls=%fused_computation.3.clone.1 | custom fusion | flops 262144 | bytes 3145856 | tf_op jit(solution)/shard_map/while/body/eval_jaxpr/scatter-add | solution.py:106
  120.4 2.4 %fusion.76 = (f32[2,4,64]{2,1,0:T(4,128)S(1)}, f32[2,1024,64,4]{1,2,3,0:T(8,128)S(1)}) fusion(f32[2,4,64,1024]{3,2,1,0:T(8,128)} %copy-done, f32[2,4,64]{2,1,0:T(4,128)S(1)} %get-tuple-element.195, bf16[1,2,64,4,128]{4,3,2,1,0:T(4,128)(2,1)S(1)} %get-tuple-element.196, bf16[4,2,1024,128]{3,2,1,0:T(8,128)(2,1)} %get-tuple-element.229, s32[]{:T(128)S(6)} %copy.84), kind=kOutput, calls=%fused_computation.7.clone.1 | convolution fusion | flops 135790080 | bytes 4853764 | tf_op jit(solution)/shard_map/while/body/eval_jaxpr/qigw,qsw->qgis/dot_general | solution.py:91
  127.7 2.1 %scatter_fusion = f32[24,8192]{1,0:T(8,128)S(1)} fusion(f32[24,8192]{1,0:T(8,128)S(1)} %get-tuple-element.211, s32[32]{0:T(128)S(1)} %fusion.73, f32[32,8192]{1,0:T(8,128)S(1)} %reshape.339), kind=kCustom, calls=%fused_computation.2.clone.1 | custom fusion | flops 262144 | bytes 3145856 | tf_op jit(solution)/shard_map/while/body/eval_jaxpr/scatter-add | solution.py:105
  131.5 4.1 %all-to-all-start = ((f32[4,4,8192]{2,1,0:T(4,128)}), f32[4,4,8192]{2,1,0:T(4,128)S(1)}, u32[]{:S(2)}, u32[]{:S(2)}) async-start(f32[4,4,8192]{2,1,0:T(4,128)} %reshape.280), calls=%async_computation | async-start | bytes 1048576 | tf_op jit(solution)/shard_map/all_to_all | solution.py:122
  137.0 8.9 %all-to-all-done = f32[4,4,8192]{2,1,0:T(4,128)S(1)} async-done(((f32[4,4,8192]{2,1,0:T(4,128)}), f32[4,4,8192]{2,1,0:T(4,128)S(1)}, u32[]{:S(2)}, u32[]{:S(2)}) %all-to-all-start) | async-done | bytes 524320 | tf_op jit(solution)/shard_map/all_to_all | solution.py:122
  146.0 3.5 %all-to-all-start.1 = ((f32[4,4,8192]{2,1,0:T(4,128)}), f32[4,4,8192]{2,1,0:T(4,128)S(1)}, u32[]{:S(2)}, u32[]{:S(2)}) async-start(f32[4,4,8192]{2,1,0:T(4,128)} %reshape.282), calls=%async_computation.1 | async-start | bytes 1048576 | tf_op jit(solution)/shard_map/all_to_all | solution.py:123
  150.7 9.0 %all-to-all-done.1 = f32[4,4,8192]{2,1,0:T(4,128)S(1)} async-done(((f32[4,4,8192]{2,1,0:T(4,128)}), f32[4,4,8192]{2,1,0:T(4,128)S(1)}, u32[]{:S(2)}, u32[]{:S(2)}) %all-to-all-start.1) | async-done | bytes 524320 | tf_op jit(solution)/shard_map/all_to_all | solution.py:123
  160.6 4.8 %all-reduce.2 = (bf16[8,8192]{1,0:T(8,128)(2,1)S(1)}, bf16[8,8192]{1,0:T(8,128)(2,1)S(1)}) all-reduce(f32[8,8192]{1,0:T(8,128)S(1)} %fusion.30, f32[8,8192]{1,0:T(8,128)S(1)} %fusion.31), channel_id=1, replica_groups=mesh['groups'=2,'seq'=4,'head'=2,'inner'=2] {'inner'}, use_global_device_ids=true, to_apply=%region_12.14 | all-reduce | flops 131072 | bytes 786432 | tf_op jit(solution)/shard_map/psum | solution.py:131
  (117 shorter events, 65.5 us)
Async XLA Ops:
  50.9 1.3 copy-start
  57.4 2.4 %copy-start.1 = (f32[2,4,64,1024]{3,2,1,0:T(8,128)S(1)}, f32[2,4,64,1024]{3,2,1,0:T(8,128)}, u32[]{:S(2)}) copy-start(f32[2,4,64,1024]{3,2,1,0:T(8,128)} %copy-done) | copy-start | bytes 6291460 | tf_op jit(solution)/shard_map/while
  71.9 1.3 copy-start
  78.4 2.4 %copy-start.1 = (f32[2,4,64,1024]{3,2,1,0:T(8,128)S(1)}, f32[2,4,64,1024]{3,2,1,0:T(8,128)}, u32[]{:S(2)}) copy-start(f32[2,4,64,1024]{3,2,1,0:T(8,128)} %copy-done) | copy-start | bytes 6291460 | tf_op jit(solution)/shard_map/while
  92.9 1.3 copy-start
  99.4 2.4 %copy-start.1 = (f32[2,4,64,1024]{3,2,1,0:T(8,128)S(1)}, f32[2,4,64,1024]{3,2,1,0:T(8,128)}, u32[]{:S(2)}) copy-start(f32[2,4,64,1024]{3,2,1,0:T(8,128)} %copy-done) | copy-start | bytes 6291460 | tf_op jit(solution)/shard_map/while
  113.9 1.3 copy-start
  120.4 2.4 %copy-start.1 = (f32[2,4,64,1024]{3,2,1,0:T(8,128)S(1)}, f32[2,4,64,1024]{3,2,1,0:T(8,128)}, u32[]{:S(2)}) copy-start(f32[2,4,64,1024]{3,2,1,0:T(8,128)} %copy-done) | copy-start | bytes 6291460 | tf_op jit(solution)/shard_map/while
  131.5 14.4 %all-to-all-start = ((f32[4,4,8192]{2,1,0:T(4,128)}), f32[4,4,8192]{2,1,0:T(4,128)S(1)}, u32[]{:S(2)}, u32[]{:S(2)}) async-start(f32[4,4,8192]{2,1,0:T(4,128)} %reshape.280), calls=%async_computation | async-start | bytes 1048576 | tf_op jit(solution)/shard_map/all_to_all | solution.py:122
  146.0 13.7 %all-to-all-start.1 = ((f32[4,4,8192]{2,1,0:T(4,128)}), f32[4,4,8192]{2,1,0:T(4,128)S(1)}, u32[]{:S(2)}, u32[]{:S(2)}) async-start(f32[4,4,8192]{2,1,0:T(4,128)} %reshape.282), calls=%async_computation.1 | async-start | bytes 1048576 | tf_op jit(solution)/shard_map/all_to_all | solution.py:123
where the time goes:
time: 168 us; the launch traced here: 167 us
  blocking collectives  39 us (23%)
  local copies, waits for them, and re-layouts  37.2 us (22%)
  matrix products  36.2 us (22%)
  other arithmetic  27.9 us (17%)
  waiting for transfers between devices  17.9 us (11%)
  starting transfers between devices  7.61 us (5%)
    all_gather x1, blocking collectives, per_device(): key_piece = lax.all_gather(keys, 'seq', axis=0, tiled=True)  17.6 us
    all_gather x1, blocking collectives, per_device(): value_piece = lax.all_gather(values, 'seq', axis=0, tiled=True)  16.6 us
    dot_general x4, matrix products, attend(): jnp.einsum('qigw,qsw->qgis', do_group, v_group, preferred_element_type=jn...  9.67 us
    all_to_all x1, waiting for transfers between devices, per_device(): lax.all_to_all(send_value_tiles, 'seq', split_axis=0, concat_axis=0, tile...  9 us
    all_to_all x1, waiting for transfers between devices, per_device(): lax.all_to_all(send_key_tiles, 'seq', split_axis=0, concat_axis=0, tiled=...  8.93 us
    scatter-add x4, other arithmetic, attend(): key_acc.at[rows_group].add(key_terms.reshape(group * TOPK, BLK * width))  8.42 us
    scatter-add x4, other arithmetic, attend(): value_acc.at[rows_group].add(value_terms.reshape(group * TOPK, BLK * width))  8.42 us
    dot_general x4, matrix products, attend(): jnp.einsum('qgis,qigw->qsw', probs_b, do_group, preferred_element_type=jn...  6.69 us
  transfers between devices with their start and end apart: 2, of which 2 were waited for; matrix products, arithmetic and copies ran while one was open for 2% of the time, Pallas kernels for 0%

commit v1 on v0

--- a/solution.py
+++ b/solution.py
@@ -49,7 +49,15 @@
     blank = jnp.zeros((blocks_here * TOPK, BLK, width), jnp.bfloat16)
     carry = (blank, blank)
     key_piece = lax.all_gather(keys, "seq", axis=0, tiled=True)
-    value_piece = lax.all_gather(values, "seq", axis=0, tiled=True)
+    value_piece = jnp.concatenate(
+        jax.lax.all_to_all(
+            jnp.stack(jax.lax.axis_size("seq") * [values]),
+            axis_name="seq",
+            split_axis=0,
+            concat_axis=0,
+        ),
+        0,
+    )
     count = key_piece.shape[0] // BLK
     relative = wanted
     inside = (relative >= 0) & (relative < count)

time: 168 us -> 164 us (0.976)
  blocking collectives: 39 us -> 26 us
  starting transfers between devices: 7.61 us -> 14.3 us
  local copies, waits for them, and re-layouts: 37.2 us -> 39 us
    all_gather x1 -> x0, blocking collectives: 16.6 us -> none  [per_device(): value_piece = lax.all_gather(values, 'seq', axis=0, tiled=True)]
    all_to_all x0 -> x1, starting transfers between devices: none -> 6.35 us  [per_device(): jax.lax.all_to_all(jnp.stack(jax.lax.axis_size('seq') * [values]), axis_n...]
    all_gather x1, blocking collectives: 17.6 us -> 21.2 us  [per_device(): key_piece = lax.all_gather(keys, 'seq', axis=0, tiled=True)]
    another operation x0 -> x1, local copies, waits for them, and re-layouts: none -> 1.8 us  [per_device(): jnp.stack(jax.lax.axis_size('seq') * [values])]
  transfers between devices with their start and end apart: 2 -> 3, of which waited for: 2 -> 2; matrix products, arithmetic and copies ran while one was open for 2% -> 5% of each run, Pallas kernels for 0% -> 0%
where the time goes in v1:
time: 164 us; the launch traced here: 163 us
  local copies, waits for them, and re-layouts  39 us (24%)
  matrix products  36.2 us (22%)
  other arithmetic  27.9 us (17%)
  blocking collectives  26 us (16%)
  waiting for transfers between devices  18.1 us (11%)
  starting transfers between devices  14.3 us (9%)
    all_gather x1, blocking collectives, per_device(): key_piece = lax.all_gather(keys, 'seq', axis=0, tiled=True)  21.2 us
    dot_general x4, matrix products, attend(): jnp.einsum('qigw,qsw->qgis', do_group, v_group, preferred_element_type=jn...  9.68 us
    all_to_all x1, waiting for transfers between devices, per_device(): lax.all_to_all(send_key_tiles, 'seq', split_axis=0, concat_axis=0, tiled=...  9.09 us
    all_to_all x1, waiting for transfers between devices, per_device(): lax.all_to_all(send_value_tiles, 'seq', split_axis=0, concat_axis=0, tile...  9 us
    scatter-add x4, other arithmetic, attend(): key_acc.at[rows_group].add(key_terms.reshape(group * TOPK, BLK * width))  8.42 us
    scatter-add x4, other arithmetic, attend(): value_acc.at[rows_group].add(value_terms.reshape(group * TOPK, BLK * width))  8.42 us
    dot_general x4, matrix products, attend(): jnp.einsum('qgis,qigw->qsw', probs_b, do_group, preferred_element_type=jn...  6.69 us
    all_to_all x1, starting transfers between devices, per_device(): jax.lax.all_to_all(jnp.stack(jax.lax.axis_size('seq') * [values]), axis_n...  6.35 us
  transfers between devices with their start and end apart: 3, of which 2 were waited for; matrix products, arithmetic and copies ran while one was open for 5% of the time, Pallas kernels for 0%

profile of v1, /device:TPU:0, one launch (start us, length us, event | category | flops | bytes accessed | tf_op | source)
XLA Modules:
  0.0 162.5 jit_solution(13147437198305870882)
XLA Ops:
  0.6 1.8 %stack.2 = bf16[4,512,1,128]{3,1,2,0:T(8,128)(2,1)} broadcast(bf16[512,128]{1,0:T(8,128)(2,1)} %bitcast.137), dimensions={1,3} | broadcast | bytes 655360 | tf_op jit(solution)/shard_map/stack | solution.py:54
  2.4 6.3 %all-to-all-start = ((bf16[4,512,1,128]{3,1,2,0:T(8,128)(2,1)}), bf16[4,512,1,128]{3,1,2,0:T(8,128)(2,1)S(1)}, u32[]{:S(2)}, u32[]{:S(2)}) async-start(bf16[4,512,1,128]{3,1,2,0:T(8,128)(2,1)} %stack.2), calls=%async_computation | async-start | bytes 1048576 | tf_op jit(solution)/shard_map/all_to_all | solution.py:53
  12.5 21.2 %all_gather.3 = bf16[2048,1,128]{2,0,1:T(8,128)(2,1)S(1)} all-gather(bf16[512,1,128]{2,0,1:T(8,128)(2,1)S(1)} %copy-done.2), channel_id=1, replica_groups=mesh['groups'=2,'seq'=4,'head'=2,'inner'=2] {'seq'}, dimensions={0}, use_global_device_ids=true | all-gather | bytes 655360 | tf_op jit(solution)/shard_map/all_gather | solution.py:51
  35.8 2.1 %gather_fusion.1 = bf16[128,64,128]{2,1,0:T(8,128)(2,1)} fusion(bf16[32,64,128]{2,1,0:T(8,128)(2,1)S(1)} %bitcast.132, s32[1024]{0:T(1024)S(1)} %pad_clamp_fusion), kind=kCustom, calls=%fused_computation.1.clone | custom fusion | bytes 4194816 | tf_op jit(solution)/shard_map/jit(_take)/gather | solution.py:66
  38.0 3.7 %select_select_fusion = (bf16[128,64,128]{2,1,0:T(8,128)(2,1)}, bf16[128,64,128]{2,1,0:T(8,128)(2,1)}) fusion(bf16[128,64,128]{2,1,0:T(8,128)(2,1)} %gather_fusion.1, pred[128]{0:T(512)(128)(4,1)S(1)} %compare_and_fusion.2, pred[128]{0:T(512)(128)(4,1)S(1)} %and.166, bf16[128,64,128]{2,1,0:T(8,128)(2,1)S(1)} %gather_fusion), kind=kLoop, calls=%fused_computation.54 | loop fusion | flops 4194304 | bytes 8388864 | tf_op jit(solution)/shard_map/jit(_where)/select_n | solution.py:68
  41.8 84.0 %while.14 = (s32[]{:T(128)}, f32[24,8192]{1,0:T(8,128)S(1)}, f32[24,8192]{1,0:T(8,128)S(1)}, bf16[4,2,64,4,128]{4,3,2,1,0:T(4,128)(2,1)}, s32[4,32]{1,0:T(4,128)...) while((s32[]{:T(128)}, f32[24,8192]{1,0:T(8,128)S(1)}, ...), condition=%wide.region_9.11_spmd, body=%wide.region_3.10_spmd.sunk | while | flops 679871104 | bytes 52703944 | solution.py:118
  50.5 2.1 %scatter_fusion.1 = f32[24,8192]{1,0:T(8,128)S(1)} fusion(f32[24,8192]{1,0:T(8,128)S(1)} %get-tuple-element.212, s32[32]{0:T(128)S(1)} %fusion.73, f32[32,8192]{1,0:T(8,128)S(1)} %reshape.343), kind=kCustom, calls=%fused_computation.3.clone.1 | custom fusion | flops 262144 | bytes 3145856 | tf_op jit(solution)/shard_map/while/body/eval_jaxpr/scatter-add | solution.py:114
  52.6 2.4 %fusion.76 = (f32[2,4,64]{2,1,0:T(4,128)S(1)}, f32[2,1024,64,4]{1,2,3,0:T(8,128)S(1)}) fusion(f32[2,4,64,1024]{3,2,1,0:T(8,128)} %copy-done, f32[2,4,64]{2,1,0:T(4,128)S(1)} %get-tuple-element.195, bf16[1,2,64,4,128]{4,3,2,1,0:T(4,128)(2,1)S(1)} %get-tuple-element.196, bf16[4,2,1024,128]{3,2,1,0:T(8,128)(2,1)} %get-tuple-element.229, s32[]{:T(128)S(6)} %copy.84), kind=kOutput, calls=%fused_computation.7.clone.1 | convolution fusion | flops 135790080 | bytes 4853764 | tf_op jit(solution)/shard_map/while/body/eval_jaxpr/qigw,qsw->qgis/dot_general | solution.py:99
  59.9 2.1 %scatter_fusion = f32[24,8192]{1,0:T(8,128)S(1)} fusion(f32[24,8192]{1,0:T(8,128)S(1)} %get-tuple-element.211, s32[32]{0:T(128)S(1)} %fusion.73, f32[32,8192]{1,0:T(8,128)S(1)} %reshape.342), kind=kCustom, calls=%fused_computation.2.clone.1 | custom fusion | flops 262144 | bytes 3145856 | tf_op jit(solution)/shard_map/while/body/eval_jaxpr/scatter-add | solution.py:113
  68.4 1.7 %convolution_bitcast_fusion.5 = f32[2,1024,128]{2,1,0:T(8,128)} fusion(bf16[1,2,64,4,128]{4,3,2,1,0:T(4,128)(2,1)S(1)} %get-tuple-element.196, f32[2,4,64,1024]{3,2,1,0:T(8,128)S(1)} %get-tuple-element.194, f32[2,4,64]{2,1,0:T(4,128)S(1)} %get-tuple-element.195), kind=kOutput, calls=%fused_computation.16.clone.1 | convolution fusion | flops 135266304 | bytes 3278848 | tf_op jit(solution)/shard_map/while/body/eval_jaxpr/qgis,qigw->qsw/dot_general | solution.py:110
  71.5 2.1 %scatter_fusion.1 = f32[24,8192]{1,0:T(8,128)S(1)} fusion(f32[24,8192]{1,0:T(8,128)S(1)} %get-tuple-element.212, s32[32]{0:T(128)S(1)} %fusion.73, f32[32,8192]{1,0:T(8,128)S(1)} %reshape.343), kind=kCustom, calls=%fused_computation.3.clone.1 | custom fusion | flops 262144 | bytes 3145856 | tf_op jit(solution)/shard_map/while/body/eval_jaxpr/scatter-add | solution.py:114
  73.6 2.4 %fusion.76 = (f32[2,4,64]{2,1,0:T(4,128)S(1)}, f32[2,1024,64,4]{1,2,3,0:T(8,128)S(1)}) fusion(f32[2,4,64,1024]{3,2,1,0:T(8,128)} %copy-done, f32[2,4,64]{2,1,0:T(4,128)S(1)} %get-tuple-element.195, bf16[1,2,64,4,128]{4,3,2,1,0:T(4,128)(2,1)S(1)} %get-tuple-element.196, bf16[4,2,1024,128]{3,2,1,0:T(8,128)(2,1)} %get-tuple-element.229, s32[]{:T(128)S(6)} %copy.84), kind=kOutput, calls=%fused_computation.7.clone.1 | convolution fusion | flops 135790080 | bytes 4853764 | tf_op jit(solution)/shard_map/while/body/eval_jaxpr/qigw,qsw->qgis/dot_general | solution.py:99
  80.9 2.1 %scatter_fusion = f32[24,8192]{1,0:T(8,128)S(1)} fusion(f32[24,8192]{1,0:T(8,128)S(1)} %get-tuple-element.211, s32[32]{0:T(128)S(1)} %fusion.73, f32[32,8192]{1,0:T(8,128)S(1)} %reshape.342), kind=kCustom, calls=%fused_computation.2.clone.1 | custom fusion | flops 262144 | bytes 3145856 | tf_op jit(solution)/shard_map/while/body/eval_jaxpr/scatter-add | solution.py:113
  92.5 2.1 %scatter_fusion.1 = f32[24,8192]{1,0:T(8,128)S(1)} fusion(f32[24,8192]{1,0:T(8,128)S(1)} %get-tuple-element.212, s32[32]{0:T(128)S(1)} %fusion.73, f32[32,8192]{1,0:T(8,128)S(1)} %reshape.343), kind=kCustom, calls=%fused_computation.3.clone.1 | custom fusion | flops 262144 | bytes 3145856 | tf_op jit(solution)/shard_map/while/body/eval_jaxpr/scatter-add | solution.py:114
  94.6 2.4 %fusion.76 = (f32[2,4,64]{2,1,0:T(4,128)S(1)}, f32[2,1024,64,4]{1,2,3,0:T(8,128)S(1)}) fusion(f32[2,4,64,1024]{3,2,1,0:T(8,128)} %copy-done, f32[2,4,64]{2,1,0:T(4,128)S(1)} %get-tuple-element.195, bf16[1,2,64,4,128]{4,3,2,1,0:T(4,128)(2,1)S(1)} %get-tuple-element.196, bf16[4,2,1024,128]{3,2,1,0:T(8,128)(2,1)} %get-tuple-element.229, s32[]{:T(128)S(6)} %copy.84), kind=kOutput, calls=%fused_computation.7.clone.1 | convolution fusion | flops 135790080 | bytes 4853764 | tf_op jit(solution)/shard_map/while/body/eval_jaxpr/qigw,qsw->qgis/dot_general | solution.py:99
  101.9 2.1 %scatter_fusion = f32[24,8192]{1,0:T(8,128)S(1)} fusion(f32[24,8192]{1,0:T(8,128)S(1)} %get-tuple-element.211, s32[32]{0:T(128)S(1)} %fusion.73, f32[32,8192]{1,0:T(8,128)S(1)} %reshape.342), kind=kCustom, calls=%fused_computation.2.clone.1 | custom fusion | flops 262144 | bytes 3145856 | tf_op jit(solution)/shard_map/while/body/eval_jaxpr/scatter-add | solution.py:113
  113.5 2.1 %scatter_fusion.1 = f32[24,8192]{1,0:T(8,128)S(1)} fusion(f32[24,8192]{1,0:T(8,128)S(1)} %get-tuple-element.212, s32[32]{0:T(128)S(1)} %fusion.73, f32[32,8192]{1,0:T(8,128)S(1)} %reshape.343), kind=kCustom, calls=%fused_computation.3.clone.1 | custom fusion | flops 262144 | bytes 3145856 | tf_op jit(solution)/shard_map/while/body/eval_jaxpr/scatter-add | solution.py:114
  115.6 2.4 %fusion.76 = (f32[2,4,64]{2,1,0:T(4,128)S(1)}, f32[2,1024,64,4]{1,2,3,0:T(8,128)S(1)}) fusion(f32[2,4,64,1024]{3,2,1,0:T(8,128)} %copy-done, f32[2,4,64]{2,1,0:T(4,128)S(1)} %get-tuple-element.195, bf16[1,2,64,4,128]{4,3,2,1,0:T(4,128)(2,1)S(1)} %get-tuple-element.196, bf16[4,2,1024,128]{3,2,1,0:T(8,128)(2,1)} %get-tuple-element.229, s32[]{:T(128)S(6)} %copy.84), kind=kOutput, calls=%fused_computation.7.clone.1 | convolution fusion | flops 135790080 | bytes 4853764 | tf_op jit(solution)/shard_map/while/body/eval_jaxpr/qigw,qsw->qgis/dot_general | solution.py:99
  122.9 2.1 %scatter_fusion = f32[24,8192]{1,0:T(8,128)S(1)} fusion(f32[24,8192]{1,0:T(8,128)S(1)} %get-tuple-element.211, s32[32]{0:T(128)S(1)} %fusion.73, f32[32,8192]{1,0:T(8,128)S(1)} %reshape.342), kind=kCustom, calls=%fused_computation.2.clone.1 | custom fusion | flops 262144 | bytes 3145856 | tf_op jit(solution)/shard_map/while/body/eval_jaxpr/scatter-add | solution.py:113
  126.7 4.4 %all-to-all-start.1 = ((f32[4,4,8192]{2,1,0:T(4,128)}), f32[4,4,8192]{2,1,0:T(4,128)S(1)}, u32[]{:S(2)}, u32[]{:S(2)}) async-start(f32[4,4,8192]{2,1,0:T(4,128)} %reshape.283), calls=%async_computation.1 | async-start | bytes 1048576 | tf_op jit(solution)/shard_map/all_to_all | solution.py:130
  132.5 9.1 %all-to-all-done.1 = f32[4,4,8192]{2,1,0:T(4,128)S(1)} async-done(((f32[4,4,8192]{2,1,0:T(4,128)}), f32[4,4,8192]{2,1,0:T(4,128)S(1)}, u32[]{:S(2)}, u32[]{:S(2)}) %all-to-all-start.1) | async-done | bytes 524320 | tf_op jit(solution)/shard_map/all_to_all | solution.py:130
  141.6 3.5 %all-to-all-start.2 = ((f32[4,4,8192]{2,1,0:T(4,128)}), f32[4,4,8192]{2,1,0:T(4,128)S(1)}, u32[]{:S(2)}, u32[]{:S(2)}) async-start(f32[4,4,8192]{2,1,0:T(4,128)} %reshape.285), calls=%async_computation.2 | async-start | bytes 1048576 | tf_op jit(solution)/shard_map/all_to_all | solution.py:131
  146.4 9.0 %all-to-all-done.2 = f32[4,4,8192]{2,1,0:T(4,128)S(1)} async-done(((f32[4,4,8192]{2,1,0:T(4,128)}), f32[4,4,8192]{2,1,0:T(4,128)S(1)}, u32[]{:S(2)}, u32[]{:S(2)}) %all-to-all-start.2) | async-done | bytes 524320 | tf_op jit(solution)/shard_map/all_to_all | solution.py:131
  156.2 4.8 %all-reduce.2 = (bf16[8,8192]{1,0:T(8,128)(2,1)S(1)}, bf16[8,8192]{1,0:T(8,128)(2,1)S(1)}) all-reduce(f32[8,8192]{1,0:T(8,128)S(1)} %fusion.30, f32[8,8192]{1,0:T(8,128)S(1)} %fusion.31), channel_id=1, replica_groups=mesh['groups'=2,'seq'=4,'head'=2,'inner'=2] {'inner'}, use_global_device_ids=true, to_apply=%region_12.14 | all-reduce | flops 131072 | bytes 786432 | tf_op jit(solution)/shard_map/psum | solution.py:139
  (121 shorter events, 67.2 us)
Async XLA Ops:
  0.6 11.8 %copy-start.2 = (bf16[512,1,128]{2,0,1:T(8,128)(2,1)S(1)}, bf16[512,1,128]{2,0,1:T(8,128)(2,1)}, u32[]{:S(2)}) copy-start(bf16[512,1,128]{2,0,1:T(8,128)(2,1)} %param.12) | copy-start | bytes 393220
  2.4 33.4 %all-to-all-start = ((bf16[4,512,1,128]{3,1,2,0:T(8,128)(2,1)}), bf16[4,512,1,128]{3,1,2,0:T(8,128)(2,1)S(1)}, u32[]{:S(2)}, u32[]{:S(2)}) async-start(bf16[4,512,1,128]{3,1,2,0:T(8,128)(2,1)} %stack.2), calls=%async_computation | async-start | bytes 1048576 | tf_op jit(solution)/shard_map/all_to_all | solution.py:53
  46.1 1.3 copy-start
  52.6 2.4 %copy-start.1 = (f32[2,4,64,1024]{3,2,1,0:T(8,128)S(1)}, f32[2,4,64,1024]{3,2,1,0:T(8,128)}, u32[]{:S(2)}) copy-start(f32[2,4,64,1024]{3,2,1,0:T(8,128)} %copy-done) | copy-start | bytes 6291460 | tf_op jit(solution)/shard_map/while
  67.1 1.3 copy-start
  73.6 2.4 %copy-start.1 = (f32[2,4,64,1024]{3,2,1,0:T(8,128)S(1)}, f32[2,4,64,1024]{3,2,1,0:T(8,128)}, u32[]{:S(2)}) copy-start(f32[2,4,64,1024]{3,2,1,0:T(8,128)} %copy-done) | copy-start | bytes 6291460 | tf_op jit(solution)/shard_map/while
  88.1 1.3 copy-start
  94.6 2.4 %copy-start.1 = (f32[2,4,64,1024]{3,2,1,0:T(8,128)S(1)}, f32[2,4,64,1024]{3,2,1,0:T(8,128)}, u32[]{:S(2)}) copy-start(f32[2,4,64,1024]{3,2,1,0:T(8,128)} %copy-done) | copy-start | bytes 6291460 | tf_op jit(solution)/shard_map/while
  109.1 1.3 copy-start
  115.6 2.4 %copy-start.1 = (f32[2,4,64,1024]{3,2,1,0:T(8,128)S(1)}, f32[2,4,64,1024]{3,2,1,0:T(8,128)}, u32[]{:S(2)}) copy-start(f32[2,4,64,1024]{3,2,1,0:T(8,128)} %copy-done) | copy-start | bytes 6291460 | tf_op jit(solution)/shard_map/while
  126.7 14.9 %all-to-all-start.1 = ((f32[4,4,8192]{2,1,0:T(4,128)}), f32[4,4,8192]{2,1,0:T(4,128)S(1)}, u32[]{:S(2)}, u32[]{:S(2)}) async-start(f32[4,4,8192]{2,1,0:T(4,128)} %reshape.283), calls=%async_computation.1 | async-start | bytes 1048576 | tf_op jit(solution)/shard_map/all_to_all | solution.py:130
  141.6 13.7 %all-to-all-start.2 = ((f32[4,4,8192]{2,1,0:T(4,128)}), f32[4,4,8192]{2,1,0:T(4,128)S(1)}, u32[]{:S(2)}, u32[]{:S(2)}) async-start(f32[4,4,8192]{2,1,0:T(4,128)} %reshape.285), calls=%async_computation.2 | async-start | bytes 1048576 | tf_op jit(solution)/shard_map/all_to_all | solution.py:131
